TPU v7x, 512 devices: a whole 4x8x8 slice. The times are simulated.
512 devices in a mesh: gx: 32 (over x, y_hi, core), gy: 16 (over z, y_lo).
Axes of the slice: x: 4, y: 8 (y_hi: 4, y_lo: 2; y = y_hi * 2 + y_lo), z: 8, core: 2. Of those that a mesh axis runs over, the one named last changes fastest.
Arguments:
- positions: float32 [3, 65536], P(None, ('gx', 'gy')), may hold values from 0 to 1
- species: int32 [65536], P(('gx', 'gy')), may hold values from 0 to 3
- neighbours: int32 [8, 65536], P(None, ('gx', 'gy')), may hold values from 0 to 639, as said below
- counts: int32 [65536], P(('gx', 'gy')), may hold values from 0 to 8, as said below
- live_atoms: int32 [512], P(('gx', 'gy')), may hold values from 64 to 128, as said below
- ghost_send: int32 [262144], P(('gx', 'gy')), may hold values from 0 to 127, as said below
- embed: float32 [128, 4], replicated, may hold values from -6 to 6
- site_energy: float32 [4], replicated, may hold values from -6 to 6
- radial_in: float32 [2, 64, 8], replicated, may hold values from -3 to 3
- radial_mid: float32 [2, 64, 64], replicated, may hold values from -1 to 1
- radial_out: float32 [2, 384, 64], replicated, may hold values from -1.5 to 1.5
- contract: float32 [2, 4, 6, 128], replicated, may hold values from -6 to 6
- mix: float32 [2, 128, 128], replicated, may hold values from -1 to 1
- skip: float32 [2, 128, 128], replicated, may hold values from -0.5 to 0.5
- read_one: float32 [128], replicated, may hold values from -1 to 1
- read_hidden: float32 [16, 128], replicated, may hold values from -1 to 1
- read_out: float32 [16], replicated, may hold values from -3 to 3
Outputs:
- energy: float32 [], replicated
- forces: float32 [3, 65536], P(None, ('gx', 'gy'))
- stress: float32 [3, 3], replicated
Inputs may be any that keep to these rules, and one draw needn't show every extreme that they name: `live_atoms`: device 0 holds 128 real atoms. `counts`: zero for padding atoms; atom slot 0 of every device uses all 8 slots. `neighbours`: the used slots of an atom name a real atom of the same device (below its live count) or a ghost slot, numbered from 128 in the order of directions. `ghost_send`: each entry names a real atom of the sending device.
All inputs are finite; a program needn't handle non-finite values.
Results may differ from a plain program's by a relative error of at most 0.0003.
Values sent between devices are 32-bit elements; how exact they have to be, the bound alone decides.
A program may use at most 64 MiB of HBM per device.

v0:
```python
import functools

import jax
import jax.numpy as jnp
from jax import lax
from jax.experimental import pallas as pl
from jax.experimental.pallas import tpu as pltpu
from jax.sharding import PartitionSpec as P

F32 = jnp.float32
BF = jnp.bfloat16
C = 128
H = 64
K = 8
A = 128
E = K * A
G = 512
DIRS = ((-1, -1), (-1, 0), (-1, 1), (0, -1), (0, 1), (1, -1), (1, 0), (1, 1))
NX, NYH, NCORE = 4, 4, 2
NZ, NYL = 8, 2
SPACING = 2.0 / 7.0


def dot(a, b):
    return lax.dot_general(a, b, (((1,), (0,)), ((), ())), preferred_element_type=F32)


def dot_nt(a, b):
    return lax.dot_general(a, b, (((1,), (1,)), ((), ())), preferred_element_type=F32)


def dot_tn(a, b):
    return lax.dot_general(a, b, (((0,), (0,)), ((), ())), preferred_element_type=F32)


def split2(x):
    hi = x.astype(BF)
    return hi, (x - hi.astype(F32)).astype(BF)


def split3(x):
    hi = x.astype(BF).astype(F32)
    rest = x - hi
    mid = rest.astype(BF).astype(F32)
    return hi, mid, rest - mid


def dot3(a, b):
    ah, al = split2(a)
    bh, bl = split2(b)
    return dot(ah, bh) + (dot(ah, bl) + dot(al, bh))


def stack3(x):
    hi, lo = split2(x)
    return jnp.concatenate([hi, lo, hi], 0)


def iota(shape, axis):
    return lax.broadcasted_iota(jnp.int32, shape, axis)


def eye(n, dtype=BF):
    return (iota((n, n), 0) == iota((n, n), 1)).astype(F32).astype(dtype)


def spread3(w):
    n = w.shape[1]
    hi, lo = split2(w)
    row, col = iota((n, 3 * n), 0), iota((n, 3 * n), 1)
    first = ((col == row) | (col == row + n)).astype(F32).astype(BF)
    last = (col == row + 2 * n).astype(F32).astype(BF)
    return (dot(hi, first) + dot(lo, last)).astype(BF)


def transpose2(w):
    hi, lo = split2(w)
    unit = eye(w.shape[1])
    return dot_nt(unit, hi).astype(BF), dot_nt(unit, lo).astype(BF)


def rows3(x):
    hi, mid, lo = split3(x)
    return jnp.concatenate([hi, mid, lo, jnp.zeros_like(hi)], 0).astype(BF)


def fold3(y):
    return y[0:8] + (y[8:16] + y[16:24])


def fold2(y):
    n = y.shape[0] // 2
    return y[:n] + y[n:]


def tile_lanes(x, count):
    return jnp.concatenate([x] * count, 1)


def twice(x):
    return jnp.concatenate([x, x], 0)


def kernel(
    live_ref, pos_ref, kind_ref, neigh_ref, count_ref, send_ref, embed_ref, site_ref, win_ref,
    wmid_ref, wout_ref, contract_ref, mix_ref, skip_ref, rone_ref, rhid_ref, rout_ref,
    energy_ref, forces_ref, stress_ref,
    s_ref, st_ref, oh_ref, oht_ref,
    snd1, rcv1, snd2, rcv2, snd3, rcv3, snd4, rcv4, ar1s, ar1r, ar2s, ar2r, ar3s, ar3r,
    rad_ref, feat_ref, hb_ref, a_ref, sel_ref, da_ref, dr_ref, gn_ref, d1_ref, d2_ref, hid_ref,
    bas_ref, wic_ref, wmc_ref, woc_ref, wot_ref, wmt_ref, wit_ref, mixc_ref, mixt_ref, mixed_ref,
    edge_ref, dh_ref,
    ss1, rs1, ss2, rs2, ss3, rs3, ss4, rs4, sa1, ra1, sa2, ra2, sa3, ra3,
):
    p = lax.axis_index("gx")
    q = lax.axis_index("gy")
    n_gx = NX * NYH * NCORE
    n_gy = NZ * NYL

    def near(ox, oy):
        return (lax.rem(p + (ox + n_gx), n_gx), lax.rem(q + (oy + n_gy), n_gy))

    core = lax.rem(p, NCORE)
    y_hi = lax.rem(lax.div(p, NCORE), NYH)
    x = lax.div(p, NCORE * NYH)
    y_lo = lax.rem(q, NYL)
    z = lax.div(q, NYL)
    y = y_hi * NYL + y_lo

    def peer_a(i):
        dx, dc = i // NCORE, i % NCORE
        return ((lax.rem(x + dx, NX) * NYH + y_hi) * NCORE + lax.rem(core + dc, NCORE), q)

    def peer_b(i):
        yy = lax.rem(y + i, NYH * NYL)
        return ((x * NYH + lax.div(yy, NYL)) * NCORE + core, z * NYL + lax.rem(yy, NYL))

    def peer_c(i):
        return (p, lax.rem(z + i, NZ) * NYL + y_lo)

    peers_a = [peer_a(i) for i in range(1, NX * NCORE)]
    peers_b = [peer_b(i) for i in range(1, NYH * NYL)]
    peers_c = [peer_c(i) for i in range(1, NZ)]
    ahead = [near(ox, oy) for ox, oy in DIRS]
    back = [near(-ox, -oy) for ox, oy in DIRS]

    barrier = pltpu.get_barrier_semaphore()
    everyone = ahead + peers_a + peers_b + peers_c
    for who in everyone:
        pl.semaphore_signal(barrier, inc=1, device_id=who, device_id_type=pl.DeviceIdType.MESH)

    def remote(src, dst, ssem, rsem, who):
        return pltpu.make_async_remote_copy(
            src_ref=src, dst_ref=dst, send_sem=ssem, recv_sem=rsem, device_id=who,
            device_id_type=pl.DeviceIdType.MESH,
        )

    half = iota((8, 128), 1) < 64

    for b in range(4):
        row = send_ref[0:1, b * 128 : (b + 1) * 128]
        s_ref[:, b * 128 : (b + 1) * 128] = (iota((A, 128), 0) == row).astype(F32).astype(BF)
    kind = kind_ref[0:1, :]
    own8 = jnp.concatenate([pos_ref[...], kind.astype(F32), jnp.zeros((4, A), F32)], 0)
    own32 = rows3(own8)
    packet = fold3(dot(own32, s_ref[...]))
    for b in range(4):
        snd1[b] = packet[:, b * 128 : (b + 1) * 128]

    pl.semaphore_wait(barrier, len(everyone))
    copies1 = [remote(snd1.at[o // 2], rcv1.at[o], ss1.at[o], rs1.at[o], back[o]) for o in range(8)]
    for copy in copies1:
        copy.start()

    for k in range(K):
        row = neigh_ref[k : k + 1, :]
        oh_ref[:, k * A : (k + 1) * A] = (iota((A + G, A), 0) == row).astype(F32).astype(BF)
    unit = eye(128)
    for k in range(K):
        for b in range(5):
            block = oh_ref[b * 128 : (b + 1) * 128, k * A : (k + 1) * A]
            oht_ref[k * A : (k + 1) * A, b * 128 : (b + 1) * 128] = dot_tn(block, unit).astype(BF)
    for b in range(4):
        st_ref[b * 128 : (b + 1) * 128, :] = dot_tn(s_ref[:, b * 128 : (b + 1) * 128], unit).astype(BF)

    kinds4 = iota((16, A), 0)
    onehot16 = ((lax.rem(kinds4, 4) == kind) & (kinds4 < 12)).astype(F32).astype(BF)
    for l in range(2):
        in_h = win_ref[l].astype(BF).astype(F32)
        in_rows = jnp.concatenate([in_h, in_h, win_ref[l] - in_h, jnp.zeros_like(in_h)], 0)
        wic_ref[l] = dot_tn(in_rows.astype(BF), eye(32)).astype(BF)
        wmc_ref[l] = spread3(wmid_ref[l])
        oh_t, ol_t = split2(wout_ref[l])
        wot_ref[l] = jnp.concatenate([oh_t, ol_t], 0)
        woc_ref[l] = dot_tn(jnp.concatenate([oh_t, oh_t, ol_t], 0), eye(3 * H)).astype(BF)
        mh_t, ml_t = transpose2(wmid_ref[l])
        wmt_ref[l] = spread3(mh_t.astype(F32) + ml_t.astype(F32))
        wit_ref[l] = spread3(win_ref[l])
        parts = []
        for path in range(6):
            hi, mid, lo = split3(contract_ref[l, path])
            parts.append(jnp.concatenate([hi, mid, lo, jnp.zeros_like(hi)], 0).astype(BF))
        sel_ref[l] = dot_tn(jnp.concatenate(parts, 1), onehot16)
    mixh, mixl = split2(mix_ref[0])
    mixc_ref[...] = jnp.concatenate([mixh, mixh, mixl], 1)
    mth, mtl = transpose2(mix_ref[0])
    mixt_ref[...] = jnp.concatenate([mth, mth, mtl], 1)
    eh, em, el = split3(embed_ref[...])
    embed_rows = jnp.concatenate([eh, em, el, jnp.zeros_like(eh)], 0).astype(BF)
    embed16 = dot_tn(embed_rows, eye(16)).astype(BF)
    start_own = dot(embed16, onehot16)
    skip_start = dot3(skip_ref[0], start_own)
    read_mix = dot3(rhid_ref[...], mix_ref[1])
    read_skip = dot3(rhid_ref[...], skip_ref[1])
    rm_h, rm_l = split2(read_mix)
    rmc = jnp.concatenate([rm_h, rm_h, rm_l], 1)
    live_row = (iota((1, A), 1) < live_ref[...]).astype(F32)
    site_row = jnp.zeros((1, A), F32)
    for s in range(4):
        site_row = jnp.where(kind == s, site_ref[0:1, s : s + 1], site_row)

    gathered = fold3(dot(own32, oh_ref[0:A, :]))
    for copy in copies1:
        copy.wait()
    blocks = []
    rows8 = iota((8, 128), 0)
    for b in range(4):
        (ax, ay), (bx, by) = DIRS[2 * b], DIRS[2 * b + 1]
        shift_x = jnp.where(half, float(ax), float(bx))
        shift_y = jnp.where(half, float(ay), float(by))
        shift = jnp.where(rows8 == 0, shift_x, jnp.where(rows8 == 1, shift_y, 0.0))
        blocks.append(jnp.where(half, rcv1[2 * b], rcv1[2 * b + 1]) + shift)
    ghosts8 = jnp.concatenate(blocks, 1)
    gathered = gathered + fold3(dot(rows3(ghosts8), oh_ref[A:, :]))
    own_base = jnp.where(rows8 < 3, own8, 0.0)
    edge = gathered - tile_lanes(own_base, K)
    edge_ref[...] = edge
    ex, ey, ez = edge[0:1], edge[1:2], edge[2:3]
    spec_row = edge[3:4]
    scaled = (ex * ex + ey * ey + ez * ez) * 0.25
    valid = jnp.concatenate([(k < count_ref[0:1, :]).astype(F32) for k in range(K)], 1)
    cut = jnp.exp(-scaled) * valid * 0.125
    offset = (scaled - iota((8, E), 0).astype(F32) * SPACING) / SPACING
    basis = jnp.exp(-0.5 * (offset * offset))
    slope = basis * (offset * (-1.0 / SPACING))
    bh = basis.astype(BF).astype(F32)
    bas_ref[...] = jnp.concatenate([bh, basis - bh, bh, jnp.zeros_like(bh)], 0).astype(BF)

    def radial(l):
        pre = dot(wic_ref[l], bas_ref[...])
        sig = jax.nn.sigmoid(pre)
        act = pre * sig
        d1_ref[l] = sig + act * (1.0 - sig)
        pre = dot(wmc_ref[l], stack3(act))
        sig = jax.nn.sigmoid(pre)
        act = pre * sig
        d2_ref[l] = sig + act * (1.0 - sig)
        hid_ref[l] = act
        rad_ref[l] = dot(woc_ref[l], stack3(act * cut))

    radial(0)
    kinds_e = iota((16, E), 0)
    onehot_e = ((lax.rem(kinds_e, 4).astype(F32) == spec_row) & (kinds_e < 12)).astype(F32).astype(BF)
    feat_ref[0] = dot(embed16, onehot_e)
    harmonics = [
        ex, ey, ez, ex * ey, ey * ez, ex * ez, 0.5 * (ex * ex - ey * ey),
        (2.0 * ez * ez - ex * ex - ey * ey) / 6.0,
    ]
    for m in range(8):
        hb_ref[m * 8 : (m + 1) * 8, :] = jnp.broadcast_to(harmonics[m], (8, E))

    def harm(m, at):
        return twice(hb_ref[m * 8 : (m + 1) * 8, at])

    def moments(l):
        def body(block, carry):
            c0 = pl.multiple_of(block * 16, 16)
            total = None
            for k in range(K):
                at = slice(k * A, (k + 1) * A)
                h = feat_ref[l, pl.ds(c0, 16), at]
                w0 = rad_ref[l, pl.ds(c0, 16), at] * h
                w1 = rad_ref[l, pl.ds(C + c0, 16), at] * h
                w2 = rad_ref[l, pl.ds(2 * C + c0, 16), at] * h
                terms = [w0]
                terms += [w1 * harm(m, at) for m in range(3)]
                terms += [w2 * harm(m, at) for m in range(3, 8)]
                total = terms if total is None else [t + u for t, u in zip(total, terms)]
            for m in range(9):
                a_ref[l, pl.ds(m * C + c0, 16), :] = total[m]
            a0, x1, y1, z1, xy, yz, xz, u, w = total
            q1 = x1 * x1 + y1 * y1 + z1 * z1
            q2 = xy * xy + yz * yz + xz * xz + u * u + w * w
            triple = (u - w) * (x1 * x1) - (u + w) * (y1 * y1) + 2.0 * w * (z1 * z1)
            triple = triple + 2.0 * (xy * (x1 * y1) + yz * (y1 * z1) + xz * (x1 * z1))
            s = [sel_ref[l, pl.ds(path * C + c0, 16), :] for path in range(6)]
            mixed = s[0] * a0 + s[1] * (a0 * a0) + s[2] * q1 + s[3] * q2 + s[4] * (a0 * q1) + s[5] * triple
            hi, lo = split2(mixed)
            mixed_ref[pl.ds(c0, 16), :] = hi
            mixed_ref[pl.ds(C + c0, 16), :] = lo
            mixed_ref[pl.ds(2 * C + c0, 16), :] = hi
            return carry

        lax.fori_loop(0, C // 16, body, 0)

    def moment_grads(l, block, dm):
        c0 = pl.multiple_of(block * 16, 16)
        a0, x1, y1, z1, xy, yz, xz, u, w = [a_ref[l, pl.ds(m * C + c0, 16), :] for m in range(9)]
        g = [dm * sel_ref[l, pl.ds(path * C + c0, 16), :] for path in range(6)]
        q1 = x1 * x1 + y1 * y1 + z1 * z1
        g5 = 2.0 * g[5]
        dq = 2.0 * (g[2] + a0 * g[4])
        g3 = 2.0 * g[3]
        return [
            g[0] + 2.0 * (a0 * g[1]) + q1 * g[4],
            x1 * dq + g5 * ((u - w) * x1 + xy * y1 + xz * z1),
            y1 * dq + g5 * (xy * x1 - (u + w) * y1 + yz * z1),
            z1 * dq + g5 * (xz * x1 + yz * y1 + 2.0 * (w * z1)),
            xy * g3 + g5 * (x1 * y1),
            yz * g3 + g5 * (y1 * z1),
            xz * g3 + g5 * (x1 * z1),
            u * g3 + g[5] * (x1 * x1 - y1 * y1),
            w * g3 + g[5] * (2.0 * (z1 * z1) - x1 * x1 - y1 * y1),
        ]

    def weight_grads(d, at):
        w1 = d[1] * harm(0, at) + d[2] * harm(1, at) + d[3] * harm(2, at)
        w2 = d[4] * harm(3, at) + d[5] * harm(4, at) + d[6] * harm(5, at)
        return d[0], w1, w2 + (d[7] * harm(6, at) + d[8] * harm(7, at))

    def radial_grads(l):
        def body(k, carry):
            at = pl.ds(pl.multiple_of(k * A, A), A)
            hs = [harm(m, at) for m in range(8)]
            acc = [jnp.zeros((16, A), F32)] * 8
            for block in range(C // 16):
                c0 = block * 16
                d = [da_ref[m * C + c0 : m * C + c0 + 16, :] for m in range(9)]
                h = feat_ref[l, c0 : c0 + 16, at]
                w1 = rad_ref[l, C + c0 : C + c0 + 16, at] * h
                w2 = rad_ref[l, 2 * C + c0 : 2 * C + c0 + 16, at] * h
                e1 = d[1] * hs[0] + d[2] * hs[1] + d[3] * hs[2]
                e2 = d[4] * hs[3] + d[5] * hs[4] + d[6] * hs[5] + (d[7] * hs[6] + d[8] * hs[7])
                for n, value in enumerate((d[0], e1, e2)):
                    hi, lo = split2(value * h)
                    dr_ref[n * C + c0 : n * C + c0 + 16, at] = hi
                    dr_ref[3 * C + n * C + c0 : 3 * C + n * C + c0 + 16, at] = lo
                acc = [acc[m] + (w1 if m < 3 else w2) * d[m + 1] for m in range(8)]
            for m in range(8):
                dh_ref[m : m + 1, at] = jnp.sum(acc[m], axis=0, keepdims=True)
            return carry

        lax.fori_loop(0, K, body, 0)
        hi_part = dot(wot_ref[l], dr_ref[0 : 3 * C, :])
        dhc = fold2(hi_part) + dot(wot_ref[l, 0:H, :], dr_ref[3 * C :, :])
        dcut = jnp.sum(dhc * hid_ref[l], axis=0, keepdims=True)
        dpre = dhc * cut * d2_ref[l]
        dpre = dot(wmt_ref[l], stack3(dpre)) * d1_ref[l]
        dbasis = dot(wit_ref[l], stack3(dpre))
        ds = jnp.sum(dbasis * slope, axis=0, keepdims=True) - cut * dcut
        ds = ds * 0.5
        g0, g1, g2, g3, g4, g5, g6, g7 = [dh_ref[m : m + 1, :] for m in range(8)]
        third = g7 * (1.0 / 3.0)
        gx = g0 + ey * g3 + ez * g5 + ex * (g6 - third + ds)
        gy = g1 + ex * g3 + ez * g4 + ey * (ds - g6 - third)
        gz = g2 + ey * g4 + ex * g5 + ez * (2.0 * third + ds)
        return jnp.concatenate([gx, gy, gz, jnp.zeros((5, E), F32)], 0)

    moments(0)
    first = dot(mixc_ref[...], mixed_ref[...]) + skip_start

    first_h, first_l = split2(first)
    first2 = jnp.concatenate([first_h, first_l], 0)
    lane64 = iota((64, 128), 1) < 64

    def pack(value, buf):
        for b in range(4):
            top = value[0:64, b * 128 : (b + 1) * 128]
            low = value[64:128, b * 128 : (b + 1) * 128]
            buf[2 * b] = jnp.where(lane64, top, pltpu.roll(low, 64, 1))
            buf[2 * b + 1] = jnp.where(lane64, pltpu.roll(top, 64, 1), low)

    def unpack(buf, b):
        one, two = buf[2 * b], buf[2 * b + 1]
        top = jnp.where(lane64, one, pltpu.roll(two, 64, 1))
        low = jnp.where(lane64, pltpu.roll(one, 64, 1), two)
        return jnp.concatenate([top, low], 0)

    def unpack_all(buf):
        return jnp.concatenate([unpack(buf, b) for b in range(4)], 1)

    pack(fold2(dot(first2, s_ref[...])), snd2)
    copies2 = [remote(snd2.at[o], rcv2.at[o], ss2.at[o], rs2.at[o], back[o]) for o in range(8)]
    for copy in copies2:
        copy.start()

    radial(1)
    feat_ref[1] = fold2(dot(first2, oh_ref[0:A, :]))
    read_base = dot3(read_skip, first)
    energy_row = live_row * (dot3(rone_ref[...], first) + site_row)

    for copy in copies2:
        copy.wait()
    gh, gl = split2(unpack_all(rcv2))
    feat_ref[1] += fold2(dot(jnp.concatenate([gh, gl], 0), oh_ref[A:, :]))

    moments(1)
    pre = dot(rmc, mixed_ref[...]) + read_base
    sig = jax.nn.sigmoid(pre)
    act = pre * sig
    rout = jnp.sum(jnp.where(iota((16, 16), 0) == iota((16, 16), 1), rout_ref[...], 0.0), axis=1, keepdims=True)
    energy_row = energy_row + live_row * jnp.sum(rout * act, axis=0, keepdims=True)
    dpre = rout * live_row * (sig + act * (1.0 - sig))
    dph, dpl = split2(dpre)
    dmixed = dot_tn(rm_h, dph) + (dot_tn(rm_h, dpl) + dot_tn(rm_l, dph))

    def neigh_body(block, carry):
        c0 = pl.multiple_of(block * 16, 16)
        d = moment_grads(1, block, da_ref[pl.ds(9 * C + c0, 16), :])
        for m in range(9):
            da_ref[pl.ds(m * C + c0, 16), :] = d[m]
        for k in range(K):
            at = slice(k * A, (k + 1) * A)
            w0, w1, w2 = weight_grads(d, at)
            g = w0 * rad_ref[1, pl.ds(c0, 16), at]
            g = g + w1 * rad_ref[1, pl.ds(C + c0, 16), at]
            g = g + w2 * rad_ref[1, pl.ds(2 * C + c0, 16), at]
            hi, lo = split2(g)
            gn_ref[pl.ds(c0, 16), at] = hi
            gn_ref[pl.ds(C + c0, 16), at] = lo
        return carry

    da_ref[9 * C :, :] = dmixed
    lax.fori_loop(0, C // 16, neigh_body, 0)
    pack(fold2(dot(gn_ref[...], oht_ref[:, A:])), snd3)
    copies3 = [remote(snd3.at[o], rcv3.at[o], ss3.at[o], rs3.at[o], ahead[o]) for o in range(8)]
    for copy in copies3:
        copy.start()

    own_grad = fold2(dot(gn_ref[...], oht_ref[:, 0:A]))
    rs_h, rs_l = split2(read_skip)
    own_grad = own_grad + dot_tn(rs_h, dph) + (dot_tn(rs_h, dpl) + dot_tn(rs_l, dph))
    o_h, o_m, o_l = split3(jnp.concatenate([rone_ref[...], jnp.zeros((7, C), F32)], 0))
    live8 = jnp.where(rows8 == 0, live_row, 0.0).astype(BF)
    own_grad = own_grad + dot_tn(o_h.astype(BF), live8)
    own_grad = own_grad + (dot_tn(o_m.astype(BF), live8) + dot_tn(o_l.astype(BF), live8))
    grad_two = radial_grads(1)

    for copy in copies3:
        copy.wait()
    rh, rl = split2(unpack_all(rcv3))
    grad_first = own_grad + fold2(dot(jnp.concatenate([rh, rl], 0), st_ref[...]))
    da_ref[9 * C :, :] = dot(mixt_ref[...], stack3(grad_first))

    def first_body(block, carry):
        c0 = pl.multiple_of(block * 16, 16)
        d = moment_grads(0, block, da_ref[pl.ds(9 * C + c0, 16), :])
        for m in range(9):
            da_ref[pl.ds(m * C + c0, 16), :] = d[m]
        return carry

    lax.fori_loop(0, C // 16, first_body, 0)
    grad = radial_grads(0) + grad_two

    sums = []
    for b in range(3):
        prod = edge * grad[b : b + 1]
        part = prod[:, 0:A]
        for k in range(1, K):
            part = part + prod[:, k * A : (k + 1) * A]
        if b == 0:
            part = jnp.where(rows8 == 3, energy_row, jnp.where(rows8 == 4, live_row, part))
        sums.append(jnp.sum(part, axis=1, keepdims=True))
    lanes8 = iota((8, 128), 1)
    total = jnp.where(lanes8 == 0, sums[0], jnp.where(lanes8 == 1, sums[1], sums[2]))
    ar1s[...] = total

    def spread(src, dst, ssem, rsem, peers):
        copies = [remote(src, dst.at[i], ssem.at[i], rsem.at[i], who) for i, who in enumerate(peers)]
        for copy in copies:
            copy.start()
        return copies

    def gather_sum(base, buf, copies):
        for i, copy in enumerate(copies):
            copy.wait()
        for i in range(len(copies)):
            base = base + buf[i]
        return base

    reduce1 = spread(ar1s, ar1r, sa1, ra1, peers_a)

    g32 = rows3(grad)
    ghost_pos = fold3(dot(g32, oht_ref[:, A:]))
    for b in range(4):
        snd4[b] = ghost_pos[:, b * 128 : (b + 1) * 128]
    copies4 = [remote(snd4.at[o // 2], rcv4.at[o], ss4.at[o], rs4.at[o], ahead[o]) for o in range(8)]
    for copy in copies4:
        copy.start()
    own_pos = fold3(dot(g32, oht_ref[:, 0:A]))
    for k in range(K):
        own_pos = own_pos - grad[:, k * A : (k + 1) * A]

    total = gather_sum(total, ar1r, reduce1)
    ar2s[...] = total
    reduce2 = spread(ar2s, ar2r, sa2, ra2, peers_b)

    for copy in copies4:
        copy.wait()
    home = jnp.concatenate([jnp.where(half, rcv4[2 * b], rcv4[2 * b + 1]) for b in range(4)], 1)
    own_pos = own_pos + fold3(dot(rows3(home), st_ref[...]))
    forces_ref[...] = -own_pos[0:3]

    total = gather_sum(total, ar2r, reduce2)
    ar3s[...] = total
    reduce3 = spread(ar3s, ar3r, sa3, ra3, peers_c)
    total = gather_sum(total, ar3r, reduce3)
    count = total[4:5, 0:1]
    energy_ref[...] = total[3:4, 0:1] / count
    stress_ref[...] = total[0:3, 0:3] / count


def per_device(
    positions, species, neighbours, counts, live_atoms, ghost_send, embed, site_energy, radial_in,
    radial_mid, radial_out, contract, mix, skip, read_one, read_hidden, read_out,
):
    vmem = pl.BlockSpec(memory_space=pltpu.VMEM)
    dma = pltpu.SemaphoreType.DMA
    energy, forces, stress = pl.pallas_call(
        kernel,
        out_shape=(
            jax.ShapeDtypeStruct((1, 1), F32),
            jax.ShapeDtypeStruct((3, A), F32),
            jax.ShapeDtypeStruct((3, 3), F32),
        ),
        in_specs=[vmem] * 17,
        out_specs=(vmem, vmem, vmem),
        scratch_shapes=[
            pltpu.VMEM((A, G), BF),
            pltpu.VMEM((G, A), BF),
            pltpu.VMEM((A + G, E), BF),
            pltpu.VMEM((E, A + G), BF),
            pltpu.VMEM((4, 8, 128), F32),
            pltpu.VMEM((8, 8, 128), F32),
            pltpu.VMEM((8, 64, 128), F32),
            pltpu.VMEM((8, 64, 128), F32),
            pltpu.VMEM((8, 64, 128), F32),
            pltpu.VMEM((8, 64, 128), F32),
            pltpu.VMEM((4, 8, 128), F32),
            pltpu.VMEM((8, 8, 128), F32),
            pltpu.VMEM((8, 128), F32),
            pltpu.VMEM((7, 8, 128), F32),
            pltpu.VMEM((8, 128), F32),
            pltpu.VMEM((7, 8, 128), F32),
            pltpu.VMEM((8, 128), F32),
            pltpu.VMEM((7, 8, 128), F32),
            pltpu.VMEM((2, 3 * C, E), F32),
            pltpu.VMEM((2, C, E), F32),
            pltpu.VMEM((64, E), F32),
            pltpu.VMEM((2, 9 * C, A), F32),
            pltpu.VMEM((2, 6 * C, A), F32),
            pltpu.VMEM((10 * C, A), F32),
            pltpu.VMEM((6 * C, E), BF),
            pltpu.VMEM((2 * C, E), BF),
            pltpu.VMEM((2, H, E), F32),
            pltpu.VMEM((2, H, E), F32),
            pltpu.VMEM((2, H, E), F32),
            pltpu.VMEM((32, E), BF),
            pltpu.VMEM((2, H, 32), BF),
            pltpu.VMEM((2, H, 3 * H), BF),
            pltpu.VMEM((2, 3 * C, 3 * H), BF),
            pltpu.VMEM((2, 2 * H, 3 * C), BF),
            pltpu.VMEM((2, H, 3 * H), BF),
            pltpu.VMEM((2, 8, 3 * H), BF),
            pltpu.VMEM((C, 3 * C), BF),
            pltpu.VMEM((C, 3 * C), BF),
            pltpu.VMEM((3 * C, A), BF),
            pltpu.VMEM((8, E), F32),
            pltpu.VMEM((8, E), F32),
            dma((8,)), dma((8,)), dma((8,)), dma((8,)), dma((8,)), dma((8,)), dma((8,)), dma((8,)),
            dma((7,)), dma((7,)), dma((7,)), dma((7,)), dma((7,)), dma((7,)),
        ],
        compiler_params=pltpu.CompilerParams(
            collective_id=0, has_side_effects=True, vmem_limit_bytes=56 * 1024 * 1024
        ),
    )(
        live_atoms.reshape(1, 1), positions, species.reshape(1, A), neighbours, counts.reshape(1, A),
        ghost_send.reshape(1, G), embed.T, site_energy.reshape(1, 4), radial_in.transpose(0, 2, 1),
        radial_mid, radial_out.transpose(0, 2, 1), contract.transpose(0, 2, 1, 3), mix, skip,
        read_one.reshape(1, C), read_hidden, read_out.reshape(1, 16),
    )
    return energy.reshape(()), forces, stress


def solution(mesh):
    both = ("gx", "gy")
    placed = (P(None, both), P(both), P(None, both), P(both), P(both), P(both)) + (P(),) * 11
    return jax.shard_map(
        per_device, mesh=mesh, in_specs=placed, out_specs=(P(), P(None, both), P()), check_vma=False
    )
```

profile of v0, /device:TPU:1, one launch (start us, length us, event | category | flops | bytes accessed | tf_op | source)
XLA Modules:
  0.0 59.3 jit_solution(4817150858603418054)
XLA Ops:
  1.3 55.0 %shard_map.184 = (f32[1,1]{1,0:T(1,128)}, f32[3,128]{1,0:T(4,128)}, f32[3,3]{1,0:T(4,128)}) custom-call(s32[1,1]{1,0:T(1,128)} %bitcast.12.live_ref, f32[3,128]{1,0:T(4,128)} %pos_ref.1, s32[1,128]{1,0:T(1,128)} %bitcast.18, s32[8,128]{1,0:T(8,128)} %neigh_ref.1, s32[1,128]{1,0:T(1,128)} %bitcast.19, s32[1,512]{1,0:T(1,128)} %bitcast.16, f32[4,128]{1,0:T(4,128)} %bitcast.17, ...), custom_call_target="tpu_custom_call" | custom-call | tf_op jit(solution)/shard_map/pallas_call | solution.py:529
  56.3 0.0 copy-start.1
  56.9 0.0 copy-done.1
  56.9 0.0 copy-start
  56.9 0.6 copy.25
  57.5 0.1 copy-done
  57.6 0.6 copy.26
Async XLA Ops:
  56.3 0.7 %copy-start.1 = (f32[3,128]{1,0:T(4,128)S(1)}, f32[3,128]{1,0:T(4,128)}, u32[]{:S(2)}) copy-start(f32[3,128]{1,0:T(4,128)} %get-tuple-element.13) | copy-start | bytes 4612
  56.9 0.7 %copy-start = (f32[3,3]{1,0:T(4,128)S(1)}, f32[3,3]{1,0:T(4,128)}, u32[]{:S(2)}) copy-start(f32[3,3]{1,0:T(4,128)} %get-tuple-element.14) | copy-start | bytes 112
where the time goes:
time: 59.6 us; the launch traced here: 59.3 us
  Pallas kernels  55 us (92%)
  between operations  3.05 us (5%)
  local copies, waits for them, and re-layouts  1.27 us (2%)
    pallas_call x1, Pallas kernels, per_device(): pl.pallas_call(kernel, out_shape=(jax.ShapeDtypeStruct((1, 1), F32), jax....  55 us
    unnamed x6, local copies, waits for them, and re-layouts  1.27 us

commit v1 on v0

--- a/solution.py
+++ b/solution.py
@@ -102,16 +102,28 @@
 
 
 def kernel(
+    live_any, pos_any, kind_any, neigh_any, count_any, send_any, embed_any, site_any, win_any,
+    wmid_any, wout_any, contract_any, mix_any, skip_any, rone_any, rhid_any, rout_any,
+    energy_ref, forces_ref, stress_ref,
     live_ref, pos_ref, kind_ref, neigh_ref, count_ref, send_ref, embed_ref, site_ref, win_ref,
     wmid_ref, wout_ref, contract_ref, mix_ref, skip_ref, rone_ref, rhid_ref, rout_ref,
-    energy_ref, forces_ref, stress_ref,
     s_ref, st_ref, oh_ref, oht_ref,
-    snd1, rcv1, snd2, rcv2, snd3, rcv3, snd4, rcv4, ar1s, ar1r, ar2s, ar2r, ar3s, ar3r,
-    rad_ref, feat_ref, hb_ref, a_ref, sel_ref, da_ref, dr_ref, gn_ref, d1_ref, d2_ref, hid_ref,
-    bas_ref, wic_ref, wmc_ref, woc_ref, wot_ref, wmt_ref, wit_ref, mixc_ref, mixt_ref, mixed_ref,
-    edge_ref, dh_ref,
-    ss1, rs1, ss2, rs2, ss3, rs3, ss4, rs4, sa1, ra1, sa2, ra2, sa3, ra3,
+    snd1, rcv1, snd2, rcv2, snd3, rcv3, snd4, rcv4, ar1s, ar1r, ar2s, ar2r,
+    rad_ref, radp_ref, feat_ref, hb_ref, a_ref, sel_ref, da_ref, gn_ref, d1_ref, d2_ref, hid_ref,
+    bas_ref, basp_ref, wic_ref, wmc_ref, woc_ref, mixc_ref, mixt_ref, mixed_ref, dh_ref, q_ref,
+    in_sem, ss1, rs1, ss2, rs2, ss3, rs3, ss4, rs4, sa1, ra1, sa2, ra2,
 ):
+    arrays = [
+        (pos_any, pos_ref), (kind_any, kind_ref), (send_any, send_ref), (neigh_any, neigh_ref),
+        (count_any, count_ref), (live_any, live_ref), (embed_any, embed_ref), (site_any, site_ref),
+        (win_any, win_ref), (wmid_any, wmid_ref), (wout_any, wout_ref), (contract_any, contract_ref),
+        (mix_any, mix_ref), (skip_any, skip_ref), (rone_any, rone_ref), (rhid_any, rhid_ref),
+        (rout_any, rout_ref),
+    ]
+    loads = [pltpu.make_async_copy(src, dst, in_sem.at[i]) for i, (src, dst) in enumerate(arrays)]
+    for load in loads[:3]:
+        load.start()
+
     p = lax.axis_index("gx")
     q = lax.axis_index("gy")
     n_gx = NX * NYH * NCORE
@@ -128,26 +140,28 @@
     y = y_hi * NYL + y_lo
 
     def peer_a(i):
-        dx, dc = i // NCORE, i % NCORE
-        return ((lax.rem(x + dx, NX) * NYH + y_hi) * NCORE + lax.rem(core + dc, NCORE), q)
+        yy = lax.rem(y + i // NCORE, NYH * NYL)
+        cc = lax.rem(core + i % NCORE, NCORE)
+        return ((x * NYH + lax.div(yy, NYL)) * NCORE + cc, z * NYL + lax.rem(yy, NYL))
 
     def peer_b(i):
-        yy = lax.rem(y + i, NYH * NYL)
-        return ((x * NYH + lax.div(yy, NYL)) * NCORE + core, z * NYL + lax.rem(yy, NYL))
-
-    def peer_c(i):
-        return (p, lax.rem(z + i, NZ) * NYL + y_lo)
-
-    peers_a = [peer_a(i) for i in range(1, NX * NCORE)]
-    peers_b = [peer_b(i) for i in range(1, NYH * NYL)]
-    peers_c = [peer_c(i) for i in range(1, NZ)]
+        xx, zz = lax.rem(x + i // NZ, NX), lax.rem(z + i % NZ, NZ)
+        return ((xx * NYH + y_hi) * NCORE + core, zz * NYL + y_lo)
+
     ahead = [near(ox, oy) for ox, oy in DIRS]
-    back = [near(-ox, -oy) for ox, oy in DIRS]
-
     barrier = pltpu.get_barrier_semaphore()
-    everyone = ahead + peers_a + peers_b + peers_c
-    for who in everyone:
+
+    def greet(who):
         pl.semaphore_signal(barrier, inc=1, device_id=who, device_id_type=pl.DeviceIdType.MESH)
+
+    for who in ahead:
+        greet(who)
+    for load in loads[3:]:
+        load.start()
+    peers_a = [peer_a(i) for i in range(1, NYH * NYL * NCORE)]
+    peers_b = [peer_b(i) for i in range(1, NX * NZ)]
+    for who in peers_a + peers_b:
+        greet(who)
 
     def remote(src, dst, ssem, rsem, who):
         return pltpu.make_async_remote_copy(
@@ -156,7 +170,20 @@
         )
 
     half = iota((8, 128), 1) < 64
-
+    sign = 2 * core - 1
+
+    def exchange(source, target, ssem, rsem, toward):
+        outer = (1 - core) * 5 if toward < 0 else core * 5
+        inner = core * 5 if toward < 0 else (1 - core) * 5
+        order = [(outer + oy + 1, sign, toward * oy) for oy in (-1, 1, 0)]
+        order += [(3, 0, -toward), (4, 0, toward)]
+        order += [(inner + oy + 1, -sign, toward * oy) for oy in (-1, 1, 0)]
+        return [
+            remote(source(o), target.at[o], ssem.at[o], rsem.at[o], near(ox, oy)) for o, ox, oy in order
+        ]
+
+    for load in loads[:3]:
+        load.wait()
     for b in range(4):
         row = send_ref[0:1, b * 128 : (b + 1) * 128]
         s_ref[:, b * 128 : (b + 1) * 128] = (iota((A, 128), 0) == row).astype(F32).astype(BF)
@@ -167,11 +194,13 @@
     for b in range(4):
         snd1[b] = packet[:, b * 128 : (b + 1) * 128]
 
-    pl.semaphore_wait(barrier, len(everyone))
-    copies1 = [remote(snd1.at[o // 2], rcv1.at[o], ss1.at[o], rs1.at[o], back[o]) for o in range(8)]
+    pl.semaphore_wait(barrier, len(ahead) + len(peers_a) + len(peers_b))
+    copies1 = exchange(lambda o: snd1.at[lax.div(o, 2)], rcv1, ss1, rs1, -1)
     for copy in copies1:
         copy.start()
 
+    for load in loads[3:]:
+        load.wait()
     for k in range(K):
         row = neigh_ref[k : k + 1, :]
         oh_ref[:, k * A : (k + 1) * A] = (iota((A + G, A), 0) == row).astype(F32).astype(BF)
@@ -191,11 +220,7 @@
         wic_ref[l] = dot_tn(in_rows.astype(BF), eye(32)).astype(BF)
         wmc_ref[l] = spread3(wmid_ref[l])
         oh_t, ol_t = split2(wout_ref[l])
-        wot_ref[l] = jnp.concatenate([oh_t, ol_t], 0)
         woc_ref[l] = dot_tn(jnp.concatenate([oh_t, oh_t, ol_t], 0), eye(3 * H)).astype(BF)
-        mh_t, ml_t = transpose2(wmid_ref[l])
-        wmt_ref[l] = spread3(mh_t.astype(F32) + ml_t.astype(F32))
-        wit_ref[l] = spread3(win_ref[l])
         parts = []
         for path in range(6):
             hi, mid, lo = split3(contract_ref[l, path])
@@ -214,6 +239,8 @@
     read_skip = dot3(rhid_ref[...], skip_ref[1])
     rm_h, rm_l = split2(read_mix)
     rmc = jnp.concatenate([rm_h, rm_h, rm_l], 1)
+    rmt = dot_tn(jnp.concatenate([rm_h, rm_h, rm_l], 0), eye(48)).astype(BF)
+    rout = jnp.sum(jnp.where(iota((16, 16), 0) == iota((16, 16), 1), rout_ref[...], 0.0), axis=1, keepdims=True)
     live_row = (iota((1, A), 1) < live_ref[...]).astype(F32)
     site_row = jnp.zeros((1, A), F32)
     for s in range(4):
@@ -234,7 +261,6 @@
     gathered = gathered + fold3(dot(rows3(ghosts8), oh_ref[A:, :]))
     own_base = jnp.where(rows8 < 3, own8, 0.0)
     edge = gathered - tile_lanes(own_base, K)
-    edge_ref[...] = edge
     ex, ey, ez = edge[0:1], edge[1:2], edge[2:3]
     spec_row = edge[3:4]
     scaled = (ex * ex + ey * ey + ez * ez) * 0.25
@@ -245,6 +271,8 @@
     slope = basis * (offset * (-1.0 / SPACING))
     bh = basis.astype(BF).astype(F32)
     bas_ref[...] = jnp.concatenate([bh, basis - bh, bh, jnp.zeros_like(bh)], 0).astype(BF)
+    bh = slope.astype(BF).astype(F32)
+    basp_ref[...] = jnp.concatenate([bh, slope - bh, bh, jnp.zeros_like(bh)], 0).astype(BF)
 
     def radial(l):
         pre = dot(wic_ref[l], bas_ref[...])
@@ -257,6 +285,11 @@
         d2_ref[l] = sig + act * (1.0 - sig)
         hid_ref[l] = act
         rad_ref[l] = dot(woc_ref[l], stack3(act * cut))
+
+    def radial_slopes(l):
+        act = dot(wic_ref[l], basp_ref[...]) * d1_ref[l]
+        act = dot(wmc_ref[l], stack3(act)) * d2_ref[l]
+        radp_ref[l] = dot(woc_ref[l], stack3((act - hid_ref[l]) * cut))
 
     radial(0)
     kinds_e = iota((16, E), 0)
@@ -332,7 +365,7 @@
         def body(k, carry):
             at = pl.ds(pl.multiple_of(k * A, A), A)
             hs = [harm(m, at) for m in range(8)]
-            acc = [jnp.zeros((16, A), F32)] * 8
+            acc = [jnp.zeros((16, A), F32)] * 9
             for block in range(C // 16):
                 c0 = block * 16
                 d = [da_ref[m * C + c0 : m * C + c0 + 16, :] for m in range(9)]
@@ -341,25 +374,16 @@
                 w2 = rad_ref[l, 2 * C + c0 : 2 * C + c0 + 16, at] * h
                 e1 = d[1] * hs[0] + d[2] * hs[1] + d[3] * hs[2]
                 e2 = d[4] * hs[3] + d[5] * hs[4] + d[6] * hs[5] + (d[7] * hs[6] + d[8] * hs[7])
-                for n, value in enumerate((d[0], e1, e2)):
-                    hi, lo = split2(value * h)
-                    dr_ref[n * C + c0 : n * C + c0 + 16, at] = hi
-                    dr_ref[3 * C + n * C + c0 : 3 * C + n * C + c0 + 16, at] = lo
-                acc = [acc[m] + (w1 if m < 3 else w2) * d[m + 1] for m in range(8)]
-            for m in range(8):
+                ds = d[0] * radp_ref[l, c0 : c0 + 16, at] + e1 * radp_ref[l, C + c0 : C + c0 + 16, at]
+                ds = ds + e2 * radp_ref[l, 2 * C + c0 : 2 * C + c0 + 16, at]
+                acc = [acc[m] + (w1 if m < 3 else w2) * d[m + 1] for m in range(8)] + [acc[8] + ds * h]
+            for m in range(9):
                 dh_ref[m : m + 1, at] = jnp.sum(acc[m], axis=0, keepdims=True)
             return carry
 
         lax.fori_loop(0, K, body, 0)
-        hi_part = dot(wot_ref[l], dr_ref[0 : 3 * C, :])
-        dhc = fold2(hi_part) + dot(wot_ref[l, 0:H, :], dr_ref[3 * C :, :])
-        dcut = jnp.sum(dhc * hid_ref[l], axis=0, keepdims=True)
-        dpre = dhc * cut * d2_ref[l]
-        dpre = dot(wmt_ref[l], stack3(dpre)) * d1_ref[l]
-        dbasis = dot(wit_ref[l], stack3(dpre))
-        ds = jnp.sum(dbasis * slope, axis=0, keepdims=True) - cut * dcut
+        g0, g1, g2, g3, g4, g5, g6, g7, ds = [dh_ref[m : m + 1, :] for m in range(9)]
         ds = ds * 0.5
-        g0, g1, g2, g3, g4, g5, g6, g7 = [dh_ref[m : m + 1, :] for m in range(8)]
         third = g7 * (1.0 / 3.0)
         gx = g0 + ey * g3 + ez * g5 + ex * (g6 - third + ds)
         gy = g1 + ex * g3 + ez * g4 + ey * (ds - g6 - third)
@@ -390,11 +414,43 @@
         return jnp.concatenate([unpack(buf, b) for b in range(4)], 1)
 
     pack(fold2(dot(first2, s_ref[...])), snd2)
-    copies2 = [remote(snd2.at[o], rcv2.at[o], ss2.at[o], rs2.at[o], back[o]) for o in range(8)]
+    copies2 = exchange(lambda o: snd2.at[o], rcv2, ss2, rs2, -1)
     for copy in copies2:
         copy.start()
 
     radial(1)
+    radial_slopes(0)
+
+    def strain_body(block, carry):
+        c0 = pl.multiple_of(block * 16, 16)
+        j0, jx, jy, jz, jxy, jyz, jxz, ju, jw = moment_grads(0, block, 1.0)
+        third = jw * (1.0 / 3.0)
+        mxx, myy, mzz = ju - third, -ju - third, 2.0 * third
+        total = None
+        for k in range(K):
+            at = slice(k * A, (k + 1) * A)
+            vx, vy, vz = harm(0, at), harm(1, at), harm(2, at)
+            h = feat_ref[0, pl.ds(c0, 16), at]
+            e1 = jx * vx + jy * vy + jz * vz
+            tx = mxx * vx + jxy * vy + jxz * vz
+            ty = jxy * vx + myy * vy + jyz * vz
+            tz = jxz * vx + jyz * vy + mzz * vz
+            e2 = 0.5 * (tx * vx + ty * vy + tz * vz)
+            u = j0 * radp_ref[0, pl.ds(c0, 16), at] + e1 * radp_ref[0, pl.ds(C + c0, 16), at]
+            u = (u + e2 * radp_ref[0, pl.ds(2 * C + c0, 16), at]) * (0.5 * h)
+            r1 = rad_ref[0, pl.ds(C + c0, 16), at] * h
+            r2 = rad_ref[0, pl.ds(2 * C + c0, 16), at] * h
+            gx = vx * u + r1 * jx + r2 * tx
+            gy = vy * u + r1 * jy + r2 * ty
+            gz = vz * u + r1 * jz + r2 * tz
+            terms = [v * g for v in (vx, vy, vz) for g in (gx, gy, gz)]
+            total = terms if total is None else [t + n for t, n in zip(total, terms)]
+        for n in range(9):
+            q_ref[pl.ds(n * C + c0, 16), :] = total[n]
+        return carry
+
+    lax.fori_loop(0, C // 16, strain_body, 0)
+    radial_slopes(1)
     feat_ref[1] = fold2(dot(first2, oh_ref[0:A, :]))
     read_base = dot3(read_skip, first)
     energy_row = live_row * (dot3(rone_ref[...], first) + site_row)
@@ -408,11 +464,10 @@
     pre = dot(rmc, mixed_ref[...]) + read_base
     sig = jax.nn.sigmoid(pre)
     act = pre * sig
-    rout = jnp.sum(jnp.where(iota((16, 16), 0) == iota((16, 16), 1), rout_ref[...], 0.0), axis=1, keepdims=True)
     energy_row = energy_row + live_row * jnp.sum(rout * act, axis=0, keepdims=True)
     dpre = rout * live_row * (sig + act * (1.0 - sig))
-    dph, dpl = split2(dpre)
-    dmixed = dot_tn(rm_h, dph) + (dot_tn(rm_h, dpl) + dot_tn(rm_l, dph))
+    dps = stack3(dpre)
+    da_ref[9 * C :, :] = dot(rmt, dps)
 
     def neigh_body(block, carry):
         c0 = pl.multiple_of(block * 16, 16)
@@ -430,27 +485,60 @@
             gn_ref[pl.ds(C + c0, 16), at] = lo
         return carry
 
-    da_ref[9 * C :, :] = dmixed
     lax.fori_loop(0, C // 16, neigh_body, 0)
     pack(fold2(dot(gn_ref[...], oht_ref[:, A:])), snd3)
-    copies3 = [remote(snd3.at[o], rcv3.at[o], ss3.at[o], rs3.at[o], ahead[o]) for o in range(8)]
+    copies3 = exchange(lambda o: snd3.at[o], rcv3, ss3, rs3, 1)
     for copy in copies3:
         copy.start()
 
     own_grad = fold2(dot(gn_ref[...], oht_ref[:, 0:A]))
     rs_h, rs_l = split2(read_skip)
-    own_grad = own_grad + dot_tn(rs_h, dph) + (dot_tn(rs_h, dpl) + dot_tn(rs_l, dph))
+    own_grad = own_grad + dot_tn(jnp.concatenate([rs_h, rs_h, rs_l], 0), dps)
     o_h, o_m, o_l = split3(jnp.concatenate([rone_ref[...], jnp.zeros((7, C), F32)], 0))
     live8 = jnp.where(rows8 == 0, live_row, 0.0).astype(BF)
     own_grad = own_grad + dot_tn(o_h.astype(BF), live8)
     own_grad = own_grad + (dot_tn(o_m.astype(BF), live8) + dot_tn(o_l.astype(BF), live8))
     grad_two = radial_grads(1)
+    dm_own = dot(mixt_ref[...], stack3(own_grad))
+    rows16, lanes16 = iota((16, 128), 0), iota((16, 128), 1)
+    partial = []
+    for a in range(3):
+        for b in range(3):
+            prod = edge[a : a + 1] * grad_two[b : b + 1]
+            part = prod[:, 0:A]
+            for k in range(1, K):
+                part = part + prod[:, k * A : (k + 1) * A]
+            partial.append(part)
+    partial = jnp.concatenate(partial + [energy_row, live_row, jnp.zeros((5, A), F32)], 0)
 
     for copy in copies3:
         copy.wait()
     rh, rl = split2(unpack_all(rcv3))
-    grad_first = own_grad + fold2(dot(jnp.concatenate([rh, rl], 0), st_ref[...]))
-    da_ref[9 * C :, :] = dot(mixt_ref[...], stack3(grad_first))
+    returned = fold2(dot(jnp.concatenate([rh, rl], 0), st_ref[...]))
+    dmixed = dot(mixt_ref[...], stack3(returned)) + dm_own
+    da_ref[9 * C :, :] = dmixed
+    for n in range(9):
+        part = jnp.sum(dmixed * q_ref[n * C : (n + 1) * C, :], axis=0, keepdims=True)
+        partial = partial + jnp.where(rows16 == n, part, 0.0)
+    sums = jnp.sum(partial, axis=1, keepdims=True)
+    total = jnp.sum(jnp.where(lanes16 == rows16, sums, 0.0), axis=0, keepdims=True)
+    ar1s[...] = total
+
+    def spread(src, dst, ssem, rsem, peers):
+        copies = [remote(src, dst.at[pl.ds(i, 1)], ssem.at[i], rsem.at[i], who) for i, who in enumerate(peers)]
+        for copy in copies:
+            copy.start()
+        return copies
+
+    def gather_sum(base, buf, copies):
+        for copy in copies:
+            copy.wait()
+        count = len(copies)
+        rows = buf[...]
+        rows = jnp.where(iota(rows.shape, 0) < count, rows, 0.0)
+        return base + jnp.sum(rows, axis=0, keepdims=True)
+
+    reduce1 = spread(ar1s, ar1r, sa1, ra1, peers_a)
 
     def first_body(block, carry):
         c0 = pl.multiple_of(block * 16, 16)
@@ -462,39 +550,11 @@
     lax.fori_loop(0, C // 16, first_body, 0)
     grad = radial_grads(0) + grad_two
 
-    sums = []
-    for b in range(3):
-        prod = edge * grad[b : b + 1]
-        part = prod[:, 0:A]
-        for k in range(1, K):
-            part = part + prod[:, k * A : (k + 1) * A]
-        if b == 0:
-            part = jnp.where(rows8 == 3, energy_row, jnp.where(rows8 == 4, live_row, part))
-        sums.append(jnp.sum(part, axis=1, keepdims=True))
-    lanes8 = iota((8, 128), 1)
-    total = jnp.where(lanes8 == 0, sums[0], jnp.where(lanes8 == 1, sums[1], sums[2]))
-    ar1s[...] = total
-
-    def spread(src, dst, ssem, rsem, peers):
-        copies = [remote(src, dst.at[i], ssem.at[i], rsem.at[i], who) for i, who in enumerate(peers)]
-        for copy in copies:
-            copy.start()
-        return copies
-
-    def gather_sum(base, buf, copies):
-        for i, copy in enumerate(copies):
-            copy.wait()
-        for i in range(len(copies)):
-            base = base + buf[i]
-        return base
-
-    reduce1 = spread(ar1s, ar1r, sa1, ra1, peers_a)
-
     g32 = rows3(grad)
     ghost_pos = fold3(dot(g32, oht_ref[:, A:]))
     for b in range(4):
         snd4[b] = ghost_pos[:, b * 128 : (b + 1) * 128]
-    copies4 = [remote(snd4.at[o // 2], rcv4.at[o], ss4.at[o], rs4.at[o], ahead[o]) for o in range(8)]
+    copies4 = exchange(lambda o: snd4.at[lax.div(o, 2)], rcv4, ss4, rs4, 1)
     for copy in copies4:
         copy.start()
     own_pos = fold3(dot(g32, oht_ref[:, 0:A]))
@@ -512,12 +572,9 @@
     forces_ref[...] = -own_pos[0:3]
 
     total = gather_sum(total, ar2r, reduce2)
-    ar3s[...] = total
-    reduce3 = spread(ar3s, ar3r, sa3, ra3, peers_c)
-    total = gather_sum(total, ar3r, reduce3)
-    count = total[4:5, 0:1]
-    energy_ref[...] = total[3:4, 0:1] / count
-    stress_ref[...] = total[0:3, 0:3] / count
+    total = total / total[:, 10:11]
+    energy_ref[...] = total[:, 9:10]
+    stress_ref[...] = jnp.concatenate([total[:, 0:3], total[:, 3:6], total[:, 6:9]], 0)
 
 
 def per_device(
@@ -526,6 +583,12 @@
 ):
     vmem = pl.BlockSpec(memory_space=pltpu.VMEM)
     dma = pltpu.SemaphoreType.DMA
+    operands = (
+        live_atoms.reshape(1, 1), positions, species.reshape(1, A), neighbours, counts.reshape(1, A),
+        ghost_send.reshape(1, G), embed.T, site_energy.reshape(1, 4), radial_in.transpose(0, 2, 1),
+        radial_mid, radial_out.transpose(0, 2, 1), contract.transpose(0, 2, 1, 3), mix, skip,
+        read_one.reshape(1, C), read_hidden, read_out.reshape(1, 16),
+    )
     energy, forces, stress = pl.pallas_call(
         kernel,
         out_shape=(
@@ -533,9 +596,10 @@
             jax.ShapeDtypeStruct((3, A), F32),
             jax.ShapeDtypeStruct((3, 3), F32),
         ),
-        in_specs=[vmem] * 17,
+        in_specs=[pl.BlockSpec(memory_space=pl.ANY)] * 17,
         out_specs=(vmem, vmem, vmem),
-        scratch_shapes=[
+        scratch_shapes=[pltpu.VMEM(value.shape, value.dtype) for value in operands]
+        + [
             pltpu.VMEM((A, G), BF),
             pltpu.VMEM((G, A), BF),
             pltpu.VMEM((A + G, E), BF),
@@ -548,47 +612,39 @@
             pltpu.VMEM((8, 64, 128), F32),
             pltpu.VMEM((4, 8, 128), F32),
             pltpu.VMEM((8, 8, 128), F32),
-            pltpu.VMEM((8, 128), F32),
-            pltpu.VMEM((7, 8, 128), F32),
-            pltpu.VMEM((8, 128), F32),
-            pltpu.VMEM((7, 8, 128), F32),
-            pltpu.VMEM((8, 128), F32),
-            pltpu.VMEM((7, 8, 128), F32),
+            pltpu.VMEM((1, 128), F32),
+            pltpu.VMEM((16, 128), F32),
+            pltpu.VMEM((1, 128), F32),
+            pltpu.VMEM((32, 128), F32),
+            pltpu.VMEM((2, 3 * C, E), F32),
             pltpu.VMEM((2, 3 * C, E), F32),
             pltpu.VMEM((2, C, E), F32),
             pltpu.VMEM((64, E), F32),
             pltpu.VMEM((2, 9 * C, A), F32),
             pltpu.VMEM((2, 6 * C, A), F32),
             pltpu.VMEM((10 * C, A), F32),
-            pltpu.VMEM((6 * C, E), BF),
             pltpu.VMEM((2 * C, E), BF),
             pltpu.VMEM((2, H, E), F32),
             pltpu.VMEM((2, H, E), F32),
             pltpu.VMEM((2, H, E), F32),
             pltpu.VMEM((32, E), BF),
+            pltpu.VMEM((32, E), BF),
             pltpu.VMEM((2, H, 32), BF),
             pltpu.VMEM((2, H, 3 * H), BF),
             pltpu.VMEM((2, 3 * C, 3 * H), BF),
-            pltpu.VMEM((2, 2 * H, 3 * C), BF),
-            pltpu.VMEM((2, H, 3 * H), BF),
-            pltpu.VMEM((2, 8, 3 * H), BF),
             pltpu.VMEM((C, 3 * C), BF),
             pltpu.VMEM((C, 3 * C), BF),
             pltpu.VMEM((3 * C, A), BF),
-            pltpu.VMEM((8, E), F32),
-            pltpu.VMEM((8, E), F32),
+            pltpu.VMEM((16, E), F32),
+            pltpu.VMEM((9 * C, A), F32),
+            dma((17,)),
             dma((8,)), dma((8,)), dma((8,)), dma((8,)), dma((8,)), dma((8,)), dma((8,)), dma((8,)),
-            dma((7,)), dma((7,)), dma((7,)), dma((7,)), dma((7,)), dma((7,)),
+            dma((15,)), dma((15,)), dma((31,)), dma((31,)),
         ],
         compiler_params=pltpu.CompilerParams(
             collective_id=0, has_side_effects=True, vmem_limit_bytes=56 * 1024 * 1024
         ),
-    )(
-        live_atoms.reshape(1, 1), positions, species.reshape(1, A), neighbours, counts.reshape(1, A),
-        ghost_send.reshape(1, G), embed.T, site_energy.reshape(1, 4), radial_in.transpose(0, 2, 1),
-        radial_mid, radial_out.transpose(0, 2, 1), contract.transpose(0, 2, 1, 3), mix, skip,
-        read_one.reshape(1, C), read_hidden, read_out.reshape(1, 16),
-    )
+    )(*operands)
     return energy.reshape(()), forces, stress
 
 

time: 59.6 us -> 56.4 us (0.946)
  Pallas kernels: 55 us -> 51.8 us
    pallas_call x1, Pallas kernels: 55 us -> 51.8 us  [per_device(): pl.pallas_call(kernel, out_shape=(jax.ShapeDtypeStruct((1, 1), F32), jax....]
where the time goes in v1:
time: 56.4 us; the launch traced here: 56.2 us
  Pallas kernels  51.8 us (92%)
  between operations  3.05 us (5%)
  local copies, waits for them, and re-layouts  1.27 us (2%)
    pallas_call x1, Pallas kernels, per_device(): pl.pallas_call(kernel, out_shape=(jax.ShapeDtypeStruct((1, 1), F32), jax....  51.8 us
    unnamed x6, local copies, waits for them, and re-layouts  1.27 us

profile of v1, /device:TPU:1, one launch (start us, length us, event | category | flops | bytes accessed | tf_op | source)
XLA Modules:
  0.0 56.2 jit_solution(8767441602987873009)
XLA Ops:
  1.3 51.8 %shard_map.184 = (f32[1,1]{1,0:T(1,128)}, f32[3,128]{1,0:T(4,128)}, f32[3,3]{1,0:T(4,128)}) custom-call(s32[1,1]{1,0:T(1,128)} %bitcast.12.live_any, f32[3,128]{1,0:T(4,128)} %pos_any.1, s32[1,128]{1,0:T(1,128)} %bitcast.18, s32[8,128]{1,0:T(8,128)} %neigh_any.1, s32[1,128]{1,0:T(1,128)} %bitcast.19, s32[1,512]{1,0:T(1,128)} %bitcast.16, f32[4,128]{1,0:T(4,128)} %bitcast.17, ...), custom_call_target="tpu_custom_call" | custom-call | tf_op jit(solution)/shard_map/pallas_call | solution.py:592
  53.1 0.0 copy-start.1
  53.8 0.0 copy-done.1
  53.8 0.0 copy-start
  53.8 0.6 %copy.25 = f32[3,128]{1,0:T(4,128)} copy(f32[3,128]{1,0:T(4,128)S(1)} %copy-done.1) | data formatting | bytes 3072
  54.4 0.1 copy-done
  54.5 0.6 %copy.26 = f32[3,3]{1,0:T(4,128)} copy(f32[3,3]{1,0:T(4,128)S(1)} %copy-done) | data formatting | bytes 72
Async XLA Ops:
  53.1 0.7 %copy-start.1 = (f32[3,128]{1,0:T(4,128)S(1)}, f32[3,128]{1,0:T(4,128)}, u32[]{:S(2)}) copy-start(f32[3,128]{1,0:T(4,128)} %get-tuple-element.13) | copy-start | bytes 4612
  53.8 0.7 %copy-start = (f32[3,3]{1,0:T(4,128)S(1)}, f32[3,3]{1,0:T(4,128)}, u32[]{:S(2)}) copy-start(f32[3,3]{1,0:T(4,128)} %get-tuple-element.14) | copy-start | bytes 112

commit v2 on v1

--- a/solution.py
+++ b/solution.py
@@ -97,6 +97,10 @@
     return jnp.concatenate([x] * count, 1)
 
 
+def lanes_at(x, index):
+    return jnp.take_along_axis(x, index, axis=1, mode="promise_in_bounds")
+
+
 def twice(x):
     return jnp.concatenate([x, x], 0)
 
@@ -104,7 +108,7 @@
 def kernel(
     live_any, pos_any, kind_any, neigh_any, count_any, send_any, embed_any, site_any, win_any,
     wmid_any, wout_any, contract_any, mix_any, skip_any, rone_any, rhid_any, rout_any,
-    energy_ref, forces_ref, stress_ref,
+    out_ref,
     live_ref, pos_ref, kind_ref, neigh_ref, count_ref, send_ref, embed_ref, site_ref, win_ref,
     wmid_ref, wout_ref, contract_ref, mix_ref, skip_ref, rone_ref, rhid_ref, rout_ref,
     s_ref, st_ref, oh_ref, oht_ref,
@@ -158,8 +162,13 @@
         greet(who)
     for load in loads[3:]:
         load.start()
-    peers_a = [peer_a(i) for i in range(1, NYH * NYL * NCORE)]
-    peers_b = [peer_b(i) for i in range(1, NX * NZ)]
+    def ring(i, n):
+        return min(i, n - i)
+
+    far_a = lambda i: (-ring(i // NCORE, NYH * NYL), i)
+    far_b = lambda i: (-ring(i // NZ, NX) - ring(i % NZ, NZ), i)
+    peers_a = [peer_a(i) for i in sorted(range(1, NYH * NYL * NCORE), key=far_a)]
+    peers_b = [peer_b(i) for i in sorted(range(1, NX * NZ), key=far_b)]
     for who in peers_a + peers_b:
         greet(who)
 
@@ -241,12 +250,11 @@
     rmc = jnp.concatenate([rm_h, rm_h, rm_l], 1)
     rmt = dot_tn(jnp.concatenate([rm_h, rm_h, rm_l], 0), eye(48)).astype(BF)
     rout = jnp.sum(jnp.where(iota((16, 16), 0) == iota((16, 16), 1), rout_ref[...], 0.0), axis=1, keepdims=True)
-    live_row = (iota((1, A), 1) < live_ref[...]).astype(F32)
+    live_row = (iota((1, A), 1) < live_ref[0]).astype(F32)
     site_row = jnp.zeros((1, A), F32)
     for s in range(4):
         site_row = jnp.where(kind == s, site_ref[0:1, s : s + 1], site_row)
 
-    gathered = fold3(dot(own32, oh_ref[0:A, :]))
     for copy in copies1:
         copy.wait()
     blocks = []
@@ -257,8 +265,15 @@
         shift_y = jnp.where(half, float(ay), float(by))
         shift = jnp.where(rows8 == 0, shift_x, jnp.where(rows8 == 1, shift_y, 0.0))
         blocks.append(jnp.where(half, rcv1[2 * b], rcv1[2 * b + 1]) + shift)
-    ghosts8 = jnp.concatenate(blocks, 1)
-    gathered = gathered + fold3(dot(rows3(ghosts8), oh_ref[A:, :]))
+    gathered = []
+    for k in range(K):
+        index = jnp.broadcast_to(neigh_ref[k : k + 1, :], (8, 128))
+        place_in, lane = lax.shift_right_logical(index, 7), lax.bitwise_and(index, 127)
+        picked = lanes_at(own8, lane)
+        for b in range(4):
+            picked = jnp.where(place_in == b + 1, lanes_at(blocks[b], lane), picked)
+        gathered.append(picked)
+    gathered = jnp.concatenate(gathered, 1)
     own_base = jnp.where(rows8 < 3, own8, 0.0)
     edge = gathered - tile_lanes(own_base, K)
     ex, ey, ez = edge[0:1], edge[1:2], edge[2:3]
@@ -569,10 +584,16 @@
         copy.wait()
     home = jnp.concatenate([jnp.where(half, rcv4[2 * b], rcv4[2 * b + 1]) for b in range(4)], 1)
     own_pos = own_pos + fold3(dot(rows3(home), st_ref[...]))
-    forces_ref[...] = -own_pos[0:3]
+    out_ref[0:3, :] = -own_pos[0:3]
 
     total = gather_sum(total, ar2r, reduce2)
     total = total / total[:, 10:11]
+    out_ref[3:4, :] = total
+
+
+def finish(out_ref, energy_ref, forces_ref, stress_ref):
+    forces_ref[...] = out_ref[0:3, :]
+    total = out_ref[3:4, :]
     energy_ref[...] = total[:, 9:10]
     stress_ref[...] = jnp.concatenate([total[:, 0:3], total[:, 3:6], total[:, 6:9]], 0)
 
@@ -584,21 +605,18 @@
     vmem = pl.BlockSpec(memory_space=pltpu.VMEM)
     dma = pltpu.SemaphoreType.DMA
     operands = (
-        live_atoms.reshape(1, 1), positions, species.reshape(1, A), neighbours, counts.reshape(1, A),
+        live_atoms, positions, species.reshape(1, A), neighbours, counts.reshape(1, A),
         ghost_send.reshape(1, G), embed.T, site_energy.reshape(1, 4), radial_in.transpose(0, 2, 1),
         radial_mid, radial_out.transpose(0, 2, 1), contract.transpose(0, 2, 1, 3), mix, skip,
         read_one.reshape(1, C), read_hidden, read_out.reshape(1, 16),
     )
-    energy, forces, stress = pl.pallas_call(
+    result = pl.pallas_call(
         kernel,
-        out_shape=(
-            jax.ShapeDtypeStruct((1, 1), F32),
-            jax.ShapeDtypeStruct((3, A), F32),
-            jax.ShapeDtypeStruct((3, 3), F32),
-        ),
+        out_shape=pltpu.VMEM((8, A), F32),
         in_specs=[pl.BlockSpec(memory_space=pl.ANY)] * 17,
-        out_specs=(vmem, vmem, vmem),
-        scratch_shapes=[pltpu.VMEM(value.shape, value.dtype) for value in operands]
+        out_specs=vmem,
+        scratch_shapes=[pltpu.SMEM((1,), jnp.int32)]
+        + [pltpu.VMEM(value.shape, value.dtype) for value in operands[1:]]
         + [
             pltpu.VMEM((A, G), BF),
             pltpu.VMEM((G, A), BF),
@@ -645,6 +663,16 @@
             collective_id=0, has_side_effects=True, vmem_limit_bytes=56 * 1024 * 1024
         ),
     )(*operands)
+    energy, forces, stress = pl.pallas_call(
+        finish,
+        out_shape=(
+            jax.ShapeDtypeStruct((1, 1), F32),
+            jax.ShapeDtypeStruct((3, A), F32),
+            jax.ShapeDtypeStruct((3, 3), F32),
+        ),
+        in_specs=[vmem],
+        out_specs=(vmem, vmem, vmem),
+    )(pltpu.with_memory_space_constraint(result, pltpu.VMEM))
     return energy.reshape(()), forces, stress
 
 

time: 56.4 us -> 53 us (0.940)
  between operations: 3.05 us -> 1.29 us
  local copies, waits for them, and re-layouts: 1.27 us -> 0 us
    unnamed x6 -> x0, local copies, waits for them, and re-layouts: 1.27 us -> none
    pallas_call x1 -> x2, Pallas kernels: 51.8 us -> 51.5 us  [the longest x1 50.9 us: per_device(): pl.pallas_call(kernel, out_shape=pltpu.VMEM((8, A), F32), in_specs=[pl.Bl...]
where the time goes in v2:
time: 53 us; the launch traced here: 52.8 us
  Pallas kernels  51.5 us (97%)
  between operations  1.29 us (2%)
    pallas_call x1, Pallas kernels, per_device(): pl.pallas_call(kernel, out_shape=pltpu.VMEM((8, A), F32), in_specs=[pl.Bl...  50.9 us

profile of v2, /device:TPU:1, one launch (start us, length us, event | category | flops | bytes accessed | tf_op | source)
XLA Modules:
  0.0 52.8 jit_solution(12941206514752375322)
XLA Ops:
  1.3 50.9 %shard_map.184.out_ref = f32[8,128]{1,0:T(8,128)S(1)} custom-call(s32[1]{0:T(128)S(6)} %copy.20.live_any, f32[3,128]{1,0:T(4,128)} %pos_any.1, s32[1,128]{1,0:T(1,128)} %bitcast.16, s32[8,128]{1,0:T(8,128)} %neigh_any.1, s32[1,128]{1,0:T(1,128)} %bitcast.17, s32[1,512]{1,0:T(1,128)} %bitcast.14, f32[4,128]{1,0:T(4,128)} %bitcast.15, f32[1,4]{1,0:T(1,128)} %bitcast.18, ...), custom_call_target="tpu_custom_call" | custom-call | tf_op jit(solution)/shard_map/pallas_call | solution.py:613
  52.2 0.7 %shard_map.185 = (f32[1,1]{1,0:T(1,128)}, f32[3,128]{1,0:T(4,128)}, f32[3,3]{1,0:T(4,128)}) custom-call(f32[8,128]{1,0:T(8,128)S(1)} %shard_map.184.out_ref), custom_call_target="tpu_custom_call" | custom-call | tf_op jit(solution)/shard_map/pallas_call | solution.py:666

commit v3 on v2

--- a/solution.py
+++ b/solution.py
@@ -180,6 +180,11 @@
 
     half = iota((8, 128), 1) < 64
     sign = 2 * core - 1
+
+    def arrive(source, target, ssem, rsem, first_slot):
+        for i in range(4):
+            o = first_slot + i
+            remote(source.at[o], target.at[o], ssem.at[o], rsem.at[o], ahead[0]).wait_recv()
 
     def exchange(source, target, ssem, rsem, toward):
         outer = (1 - core) * 5 if toward < 0 else core * 5
@@ -425,8 +430,8 @@
         low = jnp.where(lane64, pltpu.roll(one, 64, 1), two)
         return jnp.concatenate([top, low], 0)
 
-    def unpack_all(buf):
-        return jnp.concatenate([unpack(buf, b) for b in range(4)], 1)
+    def unpack_two(buf, slot):
+        return jnp.concatenate([unpack(buf, slot), unpack(buf, slot + 1)], 1)
 
     pack(fold2(dot(first2, s_ref[...])), snd2)
     copies2 = exchange(lambda o: snd2.at[o], rcv2, ss2, rs2, -1)
@@ -470,10 +475,12 @@
     read_base = dot3(read_skip, first)
     energy_row = live_row * (dot3(rone_ref[...], first) + site_row)
 
-    for copy in copies2:
-        copy.wait()
-    gh, gl = split2(unpack_all(rcv2))
-    feat_ref[1] += fold2(dot(jnp.concatenate([gh, gl], 0), oh_ref[A:, :]))
+    for group in range(2):
+        pair = (1 - core) * 2 if group == 0 else core * 2
+        arrive(snd2, rcv2, ss2, rs2, 2 * pair)
+        gh, gl = split2(unpack_two(rcv2, pair))
+        rows = pl.ds(pl.multiple_of(A + pair * 128, 128), 256)
+        feat_ref[1] += fold2(dot(jnp.concatenate([gh, gl], 0), oh_ref[rows, :]))
 
     moments(1)
     pre = dot(rmc, mixed_ref[...]) + read_base
@@ -514,7 +521,11 @@
     own_grad = own_grad + dot_tn(o_h.astype(BF), live8)
     own_grad = own_grad + (dot_tn(o_m.astype(BF), live8) + dot_tn(o_l.astype(BF), live8))
     grad_two = radial_grads(1)
-    dm_own = dot(mixt_ref[...], stack3(own_grad))
+    for n in range(3):
+        at = [q_ref[(3 * n + m) * C : (3 * n + m + 1) * C, :] for m in range(3)]
+        moved = dot(mixc_ref[...], stack3(jnp.concatenate(at, 1)))
+        for m in range(3):
+            q_ref[(3 * n + m) * C : (3 * n + m + 1) * C, :] = moved[:, m * 128 : (m + 1) * 128]
     rows16, lanes16 = iota((16, 128), 0), iota((16, 128), 1)
     partial = []
     for a in range(3):
@@ -526,14 +537,15 @@
             partial.append(part)
     partial = jnp.concatenate(partial + [energy_row, live_row, jnp.zeros((5, A), F32)], 0)
 
-    for copy in copies3:
-        copy.wait()
-    rh, rl = split2(unpack_all(rcv3))
-    returned = fold2(dot(jnp.concatenate([rh, rl], 0), st_ref[...]))
-    dmixed = dot(mixt_ref[...], stack3(returned)) + dm_own
-    da_ref[9 * C :, :] = dmixed
+    returned = own_grad
+    for group in range(2):
+        pair = core * 2 if group == 0 else (1 - core) * 2
+        arrive(snd3, rcv3, ss3, rs3, 2 * pair)
+        rh, rl = split2(unpack_two(rcv3, pair))
+        rows = pl.ds(pl.multiple_of(pair * 128, 128), 256)
+        returned = returned + fold2(dot(jnp.concatenate([rh, rl], 0), st_ref[rows, :]))
     for n in range(9):
-        part = jnp.sum(dmixed * q_ref[n * C : (n + 1) * C, :], axis=0, keepdims=True)
+        part = jnp.sum(returned * q_ref[n * C : (n + 1) * C, :], axis=0, keepdims=True)
         partial = partial + jnp.where(rows16 == n, part, 0.0)
     sums = jnp.sum(partial, axis=1, keepdims=True)
     total = jnp.sum(jnp.where(lanes16 == rows16, sums, 0.0), axis=0, keepdims=True)
@@ -554,6 +566,7 @@
         return base + jnp.sum(rows, axis=0, keepdims=True)
 
     reduce1 = spread(ar1s, ar1r, sa1, ra1, peers_a)
+    da_ref[9 * C :, :] = dot(mixt_ref[...], stack3(returned))
 
     def first_body(block, carry):
         c0 = pl.multiple_of(block * 16, 16)
@@ -588,6 +601,8 @@
 
     total = gather_sum(total, ar2r, reduce2)
     total = total / total[:, 10:11]
+    for copy in copies2 + copies3:
+        copy.wait_send()
     out_ref[3:4, :] = total
 
 

time: 53 us -> 52.9 us (level)
  no operation moved by 1% of the time
where the time goes in v3:
time: 52.9 us; the launch traced here: 52.7 us
  Pallas kernels  51.4 us (97%)
  between operations  1.29 us (2%)
    pallas_call x1, Pallas kernels, per_device(): pl.pallas_call(kernel, out_shape=pltpu.VMEM((8, A), F32), in_specs=[pl.Bl...  50.8 us

profile of v3, /device:TPU:1, one launch (start us, length us, event | category | flops | bytes accessed | tf_op | source)
XLA Modules:
  0.0 52.7 jit_solution(8286279789325480972)
XLA Ops:
  1.3 50.8 %shard_map.184.out_ref = f32[8,128]{1,0:T(8,128)S(1)} custom-call(s32[1]{0:T(128)S(6)} %copy.20.live_any, f32[3,128]{1,0:T(4,128)} %pos_any.1, s32[1,128]{1,0:T(1,128)} %bitcast.16, s32[8,128]{1,0:T(8,128)} %neigh_any.1, s32[1,128]{1,0:T(1,128)} %bitcast.17, s32[1,512]{1,0:T(1,128)} %bitcast.14, f32[4,128]{1,0:T(4,128)} %bitcast.15, f32[1,4]{1,0:T(1,128)} %bitcast.18, ...), custom_call_target="tpu_custom_call" | custom-call | tf_op jit(solution)/shard_map/pallas_call | solution.py:628
  52.1 0.7 %shard_map.185 = (f32[1,1]{1,0:T(1,128)}, f32[3,128]{1,0:T(4,128)}, f32[3,3]{1,0:T(4,128)}) custom-call(f32[8,128]{1,0:T(8,128)S(1)} %shard_map.184.out_ref), custom_call_target="tpu_custom_call" | custom-call | tf_op jit(solution)/shard_map/pallas_call | solution.py:681

commit v4 on v3

--- a/solution.py
+++ b/solution.py
@@ -559,7 +559,9 @@
 
     def gather_sum(base, buf, copies):
         for copy in copies:
-            copy.wait()
+            copy.wait_send()
+        for copy in reversed(copies):
+            copy.wait_recv()
         count = len(copies)
         rows = buf[...]
         rows = jnp.where(iota(rows.shape, 0) < count, rows, 0.0)
@@ -589,6 +591,8 @@
     for k in range(K):
         own_pos = own_pos - grad[:, k * A : (k + 1) * A]
 
+    for copy in copies2 + copies3:
+        copy.wait_send()
     total = gather_sum(total, ar1r, reduce1)
     ar2s[...] = total
     reduce2 = spread(ar2s, ar2r, sa2, ra2, peers_b)
@@ -601,8 +605,6 @@
 
     total = gather_sum(total, ar2r, reduce2)
     total = total / total[:, 10:11]
-    for copy in copies2 + copies3:
-        copy.wait_send()
     out_ref[3:4, :] = total
 
 

time: 52.9 us -> 52.7 us (level)
  no operation moved by 1% of the time
where the time goes in v4:
time: 52.7 us; the launch traced here: 52.6 us
  Pallas kernels  51.3 us (97%)
  between operations  1.29 us (2%)
    pallas_call x1, Pallas kernels, per_device(): pl.pallas_call(kernel, out_shape=pltpu.VMEM((8, A), F32), in_specs=[pl.Bl...  50.6 us

profile of v4, /device:TPU:1, one launch (start us, length us, event | category | flops | bytes accessed | tf_op | source)
XLA Modules:
  0.0 52.6 jit_solution(9239311756643744123)
XLA Ops:
  1.3 50.6 %shard_map.184.out_ref = f32[8,128]{1,0:T(8,128)S(1)} custom-call(s32[1]{0:T(128)S(6)} %copy.20.live_any, f32[3,128]{1,0:T(4,128)} %pos_any.1, s32[1,128]{1,0:T(1,128)} %bitcast.16, s32[8,128]{1,0:T(8,128)} %neigh_any.1, s32[1,128]{1,0:T(1,128)} %bitcast.17, s32[1,512]{1,0:T(1,128)} %bitcast.14, f32[4,128]{1,0:T(4,128)} %bitcast.15, f32[1,4]{1,0:T(1,128)} %bitcast.18, ...), custom_call_target="tpu_custom_call" | custom-call | tf_op jit(solution)/shard_map/pallas_call | solution.py:630
  51.9 0.7 %shard_map.185 = (f32[1,1]{1,0:T(1,128)}, f32[3,128]{1,0:T(4,128)}, f32[3,3]{1,0:T(4,128)}) custom-call(f32[8,128]{1,0:T(8,128)S(1)} %shard_map.184.out_ref), custom_call_target="tpu_custom_call" | custom-call | tf_op jit(solution)/shard_map/pallas_call | solution.py:683
